TPU v7x, 512 devices: a whole 4x8x8 slice. The times are simulated.
512 devices in a mesh: py: 32 (over y, x), pz: 16 (over z, core).
Axes of the slice: x: 4, y: 8, z: 8, core: 2. Of those that a mesh axis runs over, the one named last changes fastest.
Arguments:
- velocity: float32 [3, 320, 320, 320], P(None, 'py', 'pz'), may hold values from -12 to 12
Outputs:
- filtered_velocity: float32 [3, 128, 128, 128], P(None, 'py', 'pz')
- subgrid_stress: float32 [6, 128, 128, 128], P(None, 'py', 'pz')
All inputs are finite; a program needn't handle non-finite values.
Results may differ from a plain program's by a relative error of at most 0.000082.
Values sent between devices are 32-bit elements; how exact they have to be, the bound alone decides.
A program may use at most 128 MiB of HBM per device.

v0:
```python
import math

import jax
import jax.numpy as jnp
import numpy as np
from jax import lax
from jax.sharding import PartitionSpec as P

N = 320
M = 128

highest = lax.Precision.HIGHEST
factor_pairs = ((0, 0), (0, 1), (0, 2), (1, 1), (1, 2), (2, 2))


def filter_matrix():
    modes = np.arange(-(M // 2) + 1, M // 2)
    gain = np.exp(-(modes**2) * (2.0 * math.pi / M) ** 2 / 24.0)
    points = np.arange(M)[:, None, None] / M - np.arange(N)[None, :, None] / N
    return (np.cos(2.0 * math.pi * modes * points) * gain).sum(-1) / N


def shards(velocity):
    table = jnp.asarray(filter_matrix(), jnp.float32)
    components = [velocity[component] for component in range(3)]
    fields = jnp.stack(components + [components[a] * components[b] for a, b in factor_pairs])
    third = jnp.einsum("fyzx,mx->fyzm", fields, table, precision=highest)
    third = lax.all_to_all(third, "pz", split_axis=3, concat_axis=2, tiled=True)
    second = jnp.einsum("fyzc,mz->fymc", third, table, precision=highest)
    second = lax.all_to_all(second, "py", split_axis=2, concat_axis=1, tiled=True)
    coarse = jnp.einsum("fybc,my->fbcm", second, table, precision=highest)
    stress = jnp.stack(
        [coarse[3 + p] - coarse[a] * coarse[b] for p, (a, b) in enumerate(factor_pairs)]
    )
    return coarse[:3], stress


def solution(mesh):
    placed = P(None, "py", "pz", None)
    return jax.shard_map(
        shards, mesh=mesh, in_specs=(placed,), out_specs=(placed, placed), check_vma=False
    )
```

profile of v0, /device:TPU:1, one launch (start us, length us, event | category | flops | bytes accessed | tf_op | source)
XLA Modules:
  0.0 166.5 jit_solution(11930056360876242768)
XLA Ops:
  0.6 0.0 copy-start.2
  0.6 0.0 copy-start
  0.7 1.4 constant_dynamic-update-slice_fusion
  2.1 1.0 multiply_dynamic-update-slice_fusion.5
  3.1 0.0 copy-done
  3.3 0.0 copy-done.2
  3.3 2.9 %fusion = f32[9,10,20,128]{3,2,1,0:T(8,128)S(1)} fusion(f32[9,10,20,320]{3,2,1,0:T(8,128)S(1)} %multiply_dynamic-update-slice_fusion, f32[128,320,1,1]{0,1,3,2:T(8,128)S(1)} %copy-done.2), kind=kOutput, calls=%fused_computation.20 | convolution fusion | flops 884736000 | bytes 3389440 | tf_op jit(solution)/shard_map/fyzx,mx->fyzm/dot_general | solution.py:27
  6.2 5.8 %copy.14 = f32[9,10,20,128]{2,1,0,3:T(8,128)} copy(f32[9,10,20,128]{3,2,1,0:T(8,128)S(1)} %fusion) | data formatting | bytes 1843200 | tf_op jit(solution)/shard_map/fyzx,mx->fyzm/dot_general | solution.py:27
  12.0 7.1 %reshape.15 = f32[16,1,14400]{2,1,0:T(1,128)S(1)} reshape(f32[128,9,10,20]{3,2,1,0:T(8,128)} %bitcast.22) | data formatting | bytes 1843200
  19.1 37.4 %all_to_all.36 = f32[16,1,14400]{2,1,0:T(1,128)S(1)} all-to-all(f32[16,1,14400]{2,1,0:T(1,128)S(1)} %reshape.15), channel_id=1, replica_groups=mesh['py'=32,'pz'=16] {'pz'}, dimensions={0} | all-to-all | bytes 1843200 | tf_op jit(solution)/shard_map/all_to_all | solution.py:28
  56.5 0.5 broadcast
  57.0 3.0 %reduce = f32[16,14400]{1,0:T(8,128)S(1)} reduce(f32[16,1,14400]{2,1,0:T(1,128)S(1)} %all_to_all.36, f32[]{:T(128)} %broadcast), dimensions={1}, to_apply=%all_to_all.26.reduce_sub_computation | reduce | bytes 1843204 | tf_op jit(solution)/shard_map/all_to_all | solution.py:28
  60.0 7.9 %reshape.16 = f32[128,9,10,20]{3,2,1,0:T(8,128)} reshape(f32[16,14400]{1,0:T(8,128)S(1)} %reduce) | data formatting | bytes 1843200
  67.9 6.4 %copy.15 = f32[9,10,20,128]{3,2,1,0:T(8,128)S(1)} copy(f32[9,10,20,128]{2,1,0,3:T(8,128)} %bitcast.23) | data formatting | bytes 1843200 | tf_op jit(solution)/shard_map/all_to_all | solution.py:28
  74.2 0.0 copy-start.1
  74.2 9.8 %reshape.4 = f32[9,10,320,8]{3,2,1,0:T(8,128)} reshape(f32[9,10,20,128]{3,2,1,0:T(8,128)S(1)} %copy.15) | data formatting | bytes 1843200 | tf_op jit(solution)/shard_map/fyzc,mz->fymc/dot_general | solution.py:29
  84.0 0.0 copy-done.1
  84.0 25.7 %convolution_bitcast_fusion = f32[9,10,128,8]{2,3,1,0:T(8,128)S(1)} fusion(f32[9,10,320,8]{3,2,1,0:T(8,128)} %reshape.4, f32[128,320,1,1]{0,1,3,2:T(8,128)S(1)} %copy-done.1), kind=kOutput, calls=%fused_computation | convolution fusion | flops 353894400 | bytes 1454080 | tf_op jit(solution)/shard_map/fyzc,mz->fymc/dot_general | solution.py:29
  109.7 3.2 %copy.17 = f32[9,10,128,8]{1,3,0,2:T(8,128)} copy(f32[9,10,128,8]{2,3,1,0:T(8,128)S(1)} %convolution_bitcast_fusion) | data formatting | bytes 737280 | tf_op jit(solution)/shard_map/fyzc,mz->fymc/transpose | solution.py:29
  113.0 5.5 %reshape.17 = f32[32,1,2880]{2,1,0:T(1,128)S(1)} reshape(f32[128,9,8,10]{3,2,1,0:T(8,128)} %bitcast.25) | data formatting | bytes 737280
  118.5 24.4 %all_to_all.37 = f32[32,1,2880]{2,1,0:T(1,128)S(1)} all-to-all(f32[32,1,2880]{2,1,0:T(1,128)S(1)} %reshape.17), channel_id=1, replica_groups=mesh['py'=32,'pz'=16] {'py'}, dimensions={0} | all-to-all | bytes 737280 | tf_op jit(solution)/shard_map/all_to_all | solution.py:30
  142.9 1.5 reduce.1
  144.5 6.5 %reshape.18 = f32[128,9,8,10]{3,2,1,0:T(8,128)} reshape(f32[32,2880]{1,0:T(8,128)S(1)} %reduce.1) | data formatting | bytes 737280
  151.0 9.3 %copy.18 = f32[9,10,128,8]{0,3,2,1:T(8,128)} copy(f32[9,10,128,8]{1,3,0,2:T(8,128)} %bitcast.26) | data formatting | bytes 737280 | tf_op jit(solution)/shard_map/all_to_all | solution.py:30
  160.3 0.0 copy-start.3
  160.3 4.3 %copy.19 = f32[9,320,4,8]{1,3,2,0:T(8,128)S(1)} copy(f32[9,320,4,8]{0,3,2,1:T(8,128)} %bitcast.24) | data formatting | bytes 737280 | tf_op jit(solution)/shard_map/fybc,my->fbcm/dot_general | solution.py:31
  164.6 0.0 copy-done.3
  164.6 0.5 fusion.1
  165.1 0.6 slice.62
  165.8 0.0 copy-start.4
  165.9 0.6 copy-done.4
  (11 shorter events, 0.2 us)
Async XLA Ops:
  0.6 2.7 %copy-start.2 = (f32[128,320,1,1]{0,1,3,2:T(8,128)S(1)}, f32[128,320,1,1]{0,1,3,2:T(8,128)}, u32[]{:S(2)}) copy-start(f32[128,320,1,1]{0,1,3,2:T(8,128)} %constant.10) | copy-start | bytes 491524
  0.6 2.5 %copy-start = (f32[3,10,20,320]{3,2,1,0:T(8,128)S(1)}, f32[3,10,20,320]{3,2,1,0:T(8,128)}, u32[]{:S(2)}) copy-start(f32[3,10,20,320]{3,2,1,0:T(8,128)} %param.2) | copy-start | bytes 2304004
  74.2 9.8 %copy-start.1 = (f32[128,320,1,1]{0,1,3,2:T(8,128)S(1)}, f32[128,320,1,1]{0,1,3,2:T(8,128)}, u32[]{:S(2)}) copy-start(f32[128,320,1,1]{0,1,3,2:T(8,128)} %constant.11) | copy-start | bytes 491524
  160.3 4.3 %copy-start.3 = (f32[128,320,1,1]{0,1,3,2:T(8,128)S(1)}, f32[128,320,1,1]{0,1,3,2:T(8,128)}, u32[]{:S(2)}) copy-start(f32[128,320,1,1]{0,1,3,2:T(8,128)} %constant.12) | copy-start | bytes 491524
  165.8 0.6 copy-start.4
where the time goes:
time: 167 us; the launch traced here: 166 us
  local copies, waits for them, and re-layouts  69 us (41%)
  blocking collectives  61.9 us (37%)
  matrix products  29.1 us (17%)
  other arithmetic  5.72 us (3%)
    all_to_all x1, blocking collectives, shards(): third = lax.all_to_all(third, 'pz', split_axis=3, concat_axis=2, tiled=True)  37.4 us
    unnamed x15, local copies, waits for them, and re-layouts  29.1 us
    dot_general x1, matrix products, shards(): second = jnp.einsum('fyzc,mz->fymc', third, table, precision=highest)  25.7 us
    all_to_all x1, blocking collectives, shards(): lax.all_to_all(second, 'py', split_axis=2, concat_axis=1, tiled=True)  24.4 us
    dot_general x1, local copies, waits for them, and re-layouts, shards(): second = jnp.einsum('fyzc,mz->fymc', third, table, precision=highest)  9.79 us
    all_to_all x1, local copies, waits for them, and re-layouts, shards(): lax.all_to_all(second, 'py', split_axis=2, concat_axis=1, tiled=True)  9.29 us
    all_to_all x2, local copies, waits for them, and re-layouts, shards(): third = lax.all_to_all(third, 'pz', split_axis=3, concat_axis=2, tiled=True)  6.86 us
    dot_general x1, local copies, waits for them, and re-layouts, shards(): third = jnp.einsum('fyzx,mx->fyzm', fields, table, precision=highest)  5.81 us

commit v1 on v0

v1 whole, which is shorter than its diff:
```python
import math

import jax
import jax.numpy as jnp
import numpy as np
from jax import lax
from jax.experimental import pallas as pl
from jax.experimental.pallas import tpu as pltpu
from jax.sharding import PartitionSpec as P

N = 320
M = 128

factor_pairs = ((0, 0), (0, 1), (0, 2), (1, 1), (1, 2), (2, 2))
FIELDS = 3 + len(factor_pairs)
ROWS = 32
COLS = 16
X1 = N // ROWS
X2 = N // COLS
J = X1 // 2
M2 = M // ROWS
M3 = M // COLS
GROUP = 16
CHUNKS = 3
PIECE = 2 * X2


def filter_matrix():
    modes = np.arange(-(M // 2) + 1, M // 2)
    gain = np.exp(-(modes**2) * (2.0 * math.pi / M) ** 2 / 24.0)
    points = np.arange(M)[:, None, None] / M - np.arange(N)[None, :, None] / N
    return (np.cos(2.0 * math.pi * modes * points) * gain).sum(-1) / N


def tables():
    matrix = filter_matrix()
    blocks = matrix.reshape(ROWS, M2, COLS, X2)
    second = np.zeros((ROWS, 2, M2, COLS, 2, X2))
    for i in range(2):
        second[:, i, :, :, i, :] = blocks
    second = second.reshape(ROWS * 2 * M2, COLS * 2 * X2)
    first = matrix.T.reshape(ROWS, J, 2, M).transpose(1, 0, 2, 3)
    first = np.repeat(first[:, :, :, None, :], M2, axis=3).reshape(J, ROWS * 2 * M2, M)
    return matrix.T.copy(), second, first


def dot(a, b):
    return lax.dot_general(
        a,
        b,
        (((1,), (0,)), ((), ())),
        precision=lax.Precision.HIGHEST,
        preferred_element_type=jnp.float32,
    )


def kernel(
    v_ref,
    third_ref,
    second_hbm,
    first_hbm,
    filtered_ref,
    stress_ref,
    pairs,
    mixed,
    send_z,
    recv_z,
    send_y,
    recv_y,
    second_ref,
    first_ref,
    coarse,
    table_sem,
    send_z_sem,
    recv_z_sem,
    send_y_sem,
    recv_y_sem,
):
    py = lax.axis_index("py")
    pz = lax.axis_index("pz")
    mesh = pl.DeviceIdType.MESH

    barrier = pltpu.get_barrier_semaphore()
    for step in range(1, COLS):
        pl.semaphore_signal(
            barrier, inc=1, device_id={"pz": lax.rem(pz + step, COLS)}, device_id_type=mesh
        )
    for step in range(1, ROWS):
        pl.semaphore_signal(
            barrier, inc=1, device_id={"py": lax.rem(py + step, ROWS)}, device_id_type=mesh
        )

    second_copy = pltpu.make_async_copy(second_hbm, second_ref, table_sem.at[0])
    first_copy = pltpu.make_async_copy(first_hbm, first_ref, table_sem.at[1])
    second_copy.start()
    first_copy.start()

    for c in range(3):
        for j in range(J):
            for i in range(2):
                pairs[c, j, i * X2 : (i + 1) * X2, :] = v_ref[c, 2 * j + i]
    mixed[J * FIELDS :] = jnp.zeros((CHUNKS * GROUP - J * FIELDS, PIECE, M), jnp.float32)
    lanes = lax.broadcasted_iota(jnp.int32, (8, M), 1)

    def third_step(j):
        parts = [pairs[c, j] for c in range(3)]
        parts = parts + [parts[a] * parts[b] for a, b in factor_pairs]
        done = dot(jnp.concatenate(parts, axis=0), third_ref[...])
        mixed[j * FIELDS : (j + 1) * FIELDS] = done.reshape(FIELDS, PIECE, M)

    def spread(c):
        for r in range(PIECE // 8):
            tiles = [mixed[c * GROUP + k, 8 * r : 8 * r + 8, :] for k in range(GROUP)]
            for b in (8, 4, 2, 1):
                low = (lanes // (M3 * b)) % 2 == 0
                for k in range(GROUP):
                    if k & b == 0:
                        x, y = tiles[k], tiles[k + b]
                        tiles[k] = jnp.where(low, x, pltpu.roll(y, M3 * b, 1))
                        tiles[k + b] = jnp.where(low, pltpu.roll(x, M - M3 * b, 1), y)
            for t in range(COLS):
                send_z[c, t, 8 * r : 8 * r + 8, :] = tiles[t]

    def copy_z(c, step):
        target = lax.rem(pz + step, COLS)
        return pltpu.make_async_remote_copy(
            src_ref=send_z.at[c, target],
            dst_ref=recv_z.at[c, pz],
            send_sem=send_z_sem.at[c],
            recv_sem=recv_z_sem.at[c],
            device_id={"pz": target},
            device_id_type=mesh,
        )

    def copy_y(c, step):
        target = lax.rem(py + step, ROWS)
        return pltpu.make_async_remote_copy(
            src_ref=send_y.at[c, target],
            dst_ref=recv_y.at[c, py],
            send_sem=send_y_sem.at[c],
            recv_sem=recv_y_sem.at[c],
            device_id={"py": target},
            device_id_type=mesh,
        )

    def all_z(c):
        return pltpu.make_async_remote_copy(
            src_ref=send_z.at[c, pl.ds(0, COLS - 1)],
            dst_ref=recv_z.at[c, pl.ds(0, COLS - 1)],
            send_sem=send_z_sem.at[c],
            recv_sem=recv_z_sem.at[c],
            device_id={"pz": lax.rem(pz + 1, COLS)},
            device_id_type=mesh,
        )

    def all_y(c):
        return pltpu.make_async_remote_copy(
            src_ref=send_y.at[c, pl.ds(0, ROWS - 1)],
            dst_ref=recv_y.at[c, pl.ds(0, ROWS - 1)],
            send_sem=send_y_sem.at[c],
            recv_sem=recv_y_sem.at[c],
            device_id={"py": lax.rem(py + 1, ROWS)},
            device_id_type=mesh,
        )

    done_j = 0
    for c in range(CHUNKS):
        while done_j < J and done_j * FIELDS < (c + 1) * GROUP:
            third_step(done_j)
            done_j += 1
        spread(c)
        if c == 0:
            pl.semaphore_wait(barrier, COLS + ROWS - 2)
        for step in range(1, COLS):
            copy_z(c, step).start()
        recv_z[c, pz] = send_z[c, pz]

    coarse[...] = jnp.zeros_like(coarse)
    second_copy.wait()
    for c in range(CHUNKS):
        all_z(c).wait_recv()
        done = dot(second_ref[...], recv_z[c].reshape(COLS * PIECE, M))
        send_y[c] = done.reshape(ROWS, 2 * M2, M)
        for step in range(1, ROWS):
            copy_y(c, step).start()
        recv_y[c, py] = send_y[c, py]

    first_copy.wait()
    for c in range(CHUNKS):
        all_y(c).wait_recv()
        turned = recv_y[c].reshape(ROWS * 2 * M2, M).T
        for j in range(J):
            begin = max(j * FIELDS, c * GROUP)
            end = min((j + 1) * FIELDS, (c + 1) * GROUP)
            if begin >= end:
                continue
            rows = turned[M3 * (begin - c * GROUP) : M3 * (end - c * GROUP)]
            mask_of = lax.rem(lax.broadcasted_iota(jnp.int32, rows.shape, 1), M2)
            stacked = jnp.concatenate(
                [jnp.where(mask_of == m, rows, 0.0) for m in range(M2)], axis=0
            )
            done = dot(stacked, first_ref[j])
            fields = end - begin
            coarse[:, begin - j * FIELDS : end - j * FIELDS] += done.reshape(M2, fields, M3, M)

    for m in range(M2):
        parts = [coarse[m, f] for f in range(FIELDS)]
        for f in range(3):
            filtered_ref[f, m] = parts[f]
        for p, (a, b) in enumerate(factor_pairs):
            stress_ref[p, m] = parts[3 + p] - parts[a] * parts[b]

    for c in range(CHUNKS):
        all_z(c).wait_send()
        all_y(c).wait_send()


def shards(velocity):
    third, second, first = (jnp.asarray(table, jnp.float32) for table in tables())
    vmem = pl.BlockSpec(memory_space=pltpu.VMEM)
    anywhere = pl.BlockSpec(memory_space=pl.ANY)
    f32 = jnp.float32
    return pl.pallas_call(
        kernel,
        out_shape=(
            jax.ShapeDtypeStruct((3, M2, M3, M), f32),
            jax.ShapeDtypeStruct((6, M2, M3, M), f32),
        ),
        in_specs=[vmem, vmem, anywhere, anywhere],
        out_specs=(vmem, vmem),
        scratch_shapes=[
            pltpu.VMEM((3, J, PIECE, N), f32),
            pltpu.VMEM((CHUNKS * GROUP, PIECE, M), f32),
            pltpu.VMEM((CHUNKS, COLS, PIECE, M), f32),
            pltpu.VMEM((CHUNKS, COLS, PIECE, M), f32),
            pltpu.VMEM((CHUNKS, ROWS, 2 * M2, M), f32),
            pltpu.VMEM((CHUNKS, ROWS, 2 * M2, M), f32),
            pltpu.VMEM((ROWS * 2 * M2, COLS * PIECE), f32),
            pltpu.VMEM((J, ROWS * 2 * M2, M), f32),
            pltpu.VMEM((M2, FIELDS, M3, M), f32),
            pltpu.SemaphoreType.DMA((2,)),
            pltpu.SemaphoreType.DMA((CHUNKS,)),
            pltpu.SemaphoreType.DMA((CHUNKS,)),
            pltpu.SemaphoreType.DMA((CHUNKS,)),
            pltpu.SemaphoreType.DMA((CHUNKS,)),
        ],
        compiler_params=pltpu.CompilerParams(collective_id=0, has_side_effects=True),
    )(velocity, third, second, first)


def solution(mesh):
    placed = P(None, "py", "pz", None)
    return jax.shard_map(
        shards, mesh=mesh, in_specs=(placed,), out_specs=(placed, placed), check_vma=False
    )
```

time: 167 us -> 53.6 us (0.32)
  local copies, waits for them, and re-layouts: 69 us -> 2.96 us
  blocking collectives: 61.9 us -> 0 us
  Pallas kernels: 0 us -> 49.8 us
  matrix products: 29.1 us -> 0 us
  other arithmetic: 5.72 us -> 0 us
    all_to_all x2 -> x0, blocking collectives: 61.9 us -> none  [the longest x1 37.4 us: shards(): third = lax.all_to_all(third, 'pz', split_axis=3, concat_axis=2, tiled=True)]
    pallas_call x0 -> x1, Pallas kernels: none -> 49.8 us  [shards(): pl.pallas_call(kernel, out_shape=(jax.ShapeDtypeStruct((3, M2, M3, M), f3...]
    dot_general x3 -> x0, matrix products: 29.1 us -> none  [the longest x1 25.7 us: shards(): second = jnp.einsum('fyzc,mz->fymc', third, table, precision=highest)]
    unnamed x15 -> x2, local copies, waits for them, and re-layouts: 29.1 us -> 2.96 us
    dot_general x3 -> x0, local copies, waits for them, and re-layouts: 19.9 us -> none  [the longest x1 9.79 us: shards(): second = jnp.einsum('fyzc,mz->fymc', third, table, precision=highest)]
    all_to_all x3 -> x0, local copies, waits for them, and re-layouts: 16.2 us -> none  [the longest x1 9.29 us: shards(): lax.all_to_all(second, 'py', split_axis=2, concat_axis=1, tiled=True)]
    all_to_all x2 -> x0, other arithmetic: 4.49 us -> none  [the longest x1 2.95 us: shards(): third = lax.all_to_all(third, 'pz', split_axis=3, concat_axis=2, tiled=True)]
    transpose x1 -> x0, local copies, waits for them, and re-layouts: 3.23 us -> none  [shards(): second = jnp.einsum('fyzc,mz->fymc', third, table, precision=highest)]
where the time goes in v1:
time: 53.6 us; the launch traced here: 53.4 us
  Pallas kernels  49.8 us (93%)
  local copies, waits for them, and re-layouts  2.96 us (6%)
  between operations  0.64 us (1%)
    pallas_call x1, Pallas kernels, shards(): pl.pallas_call(kernel, out_shape=(jax.ShapeDtypeStruct((3, M2, M3, M), f3...  49.8 us
    unnamed x2, local copies, waits for them, and re-layouts  2.96 us

profile of v1, /device:TPU:1, one launch (start us, length us, event | category | flops | bytes accessed | tf_op | source)
XLA Modules:
  0.0 53.4 jit_solution(13523620645663633139)
XLA Ops:
  0.6 49.8 %shard_map.59 = (f32[3,4,8,128]{3,2,1,0:T(8,128)}, f32[6,4,8,128]{3,2,1,0:T(8,128)}) custom-call(f32[3,10,20,320]{3,2,1,0:T(8,128)} %v_ref.1, f32[320,128]{1,0:T(8,128)} %constant.6.clone.third_ref, f32[256,640]{1,0:T(8,128)} %constant.7.clone.second_hbm, f32[5,256,128]{2,1,0:T(8,128)} %constant.8.clone.first_hbm), custom_call_target="tpu_custom_call" | custom-call | tf_op jit(solution)/shard_map/pallas_call | solution.py:223
  50.4 1.4 %copy.8 = f32[3,4,8,128]{3,2,1,0:T(8,128)} copy(f32[3,4,8,128]{3,2,1,0:T(8,128)} %get-tuple-element.4) | data formatting | bytes 98304
  51.8 1.5 %copy.9 = f32[6,4,8,128]{3,2,1,0:T(8,128)} copy(f32[6,4,8,128]{3,2,1,0:T(8,128)} %get-tuple-element.5) | data formatting | bytes 196608

commit v2 on v1

v2 whole, which is shorter than its diff:
```python
import math

import jax
import jax.numpy as jnp
import numpy as np
from jax import lax
from jax.experimental import pallas as pl
from jax.experimental.pallas import tpu as pltpu
from jax.sharding import PartitionSpec as P

N = 320
M = 128

factor_pairs = ((0, 0), (0, 1), (0, 2), (1, 1), (1, 2), (2, 2))
FIELDS = 3 + len(factor_pairs)
ROWS = 32
COLS = 16
X1 = N // ROWS
X2 = N // COLS
X2P = 24
M2 = M // ROWS
M3 = M // COLS
GROUP = 16
CHUNKS = -(-X1 * FIELDS // GROUP)
PLANES = (0, 1, 3, 2, 7, 4, 6, 5)


def filter_matrix():
    modes = np.arange(-(M // 2) + 1, M // 2)
    gain = np.exp(-(modes**2) * (2.0 * math.pi / M) ** 2 / 24.0)
    points = np.arange(M)[:, None, None] / M - np.arange(N)[None, :, None] / N
    return (np.cos(2.0 * math.pi * modes * points) * gain).sum(-1) / N


def tables():
    matrix = filter_matrix()
    second = np.zeros((M, COLS, X2P))
    second[:, :, :X2] = matrix.reshape(M, COLS, X2)
    first = np.repeat(matrix.T.reshape(ROWS, X1, M).transpose(1, 0, 2), M2, axis=1)
    return matrix.T.copy(), second.reshape(M, COLS * X2P), first


def dot(a, b):
    return lax.dot_general(
        a,
        b,
        (((1,), (0,)), ((), ())),
        precision=lax.Precision.HIGH,
        preferred_element_type=jnp.float32,
    )


def kernel(
    v_hbm,
    third_hbm,
    second_hbm,
    first_hbm,
    coarse_ref,
    v_ref,
    third_ref,
    second_ref,
    first_ref,
    mixed,
    send_z,
    recv_z,
    send_y,
    recv_y,
    v_sem,
    table_sem,
    send_z_sem,
    recv_z_sem,
    send_y_sem,
    recv_y_sem,
):
    py = lax.axis_index("py")
    pz = lax.axis_index("pz")
    mesh = pl.DeviceIdType.MESH

    v_copies = [
        pltpu.make_async_copy(v_hbm.at[:, x], v_ref.at[:, x], v_sem.at[x]) for x in range(X1)
    ]
    third_copy = pltpu.make_async_copy(third_hbm, third_ref, table_sem.at[0])
    second_copy = pltpu.make_async_copy(second_hbm, second_ref, table_sem.at[1])
    first_copy = pltpu.make_async_copy(first_hbm, first_ref, table_sem.at[2])
    third_copy.start()
    for copy in v_copies:
        copy.start()
    second_copy.start()
    first_copy.start()

    barrier = pltpu.get_barrier_semaphore()
    for step in range(1, COLS):
        pl.semaphore_signal(
            barrier, inc=1, device_id={"pz": lax.rem(pz + step, COLS)}, device_id_type=mesh
        )
    for step in range(1, ROWS):
        pl.semaphore_signal(
            barrier, inc=1, device_id={"py": lax.rem(py + step, ROWS)}, device_id_type=mesh
        )

    mixed[X1 * FIELDS :] = jnp.zeros((CHUNKS * GROUP - X1 * FIELDS, X2P, M), jnp.float32)
    recv_z[:, :, X2:, :] = jnp.zeros((CHUNKS, COLS, X2P - X2, M), jnp.float32)
    lanes = lax.broadcasted_iota(jnp.int32, (8, M), 1)

    def third_step(x):
        v_copies[x].wait()
        pad = jnp.zeros((X2P - X2, N), jnp.float32)
        parts = [jnp.concatenate([v_ref[c, x], pad], axis=0) for c in range(3)]
        parts = parts + [parts[a] * parts[b] for a, b in factor_pairs]
        done = dot(jnp.concatenate(parts, axis=0), third_ref[...])
        mixed[x * FIELDS : (x + 1) * FIELDS] = done.reshape(FIELDS, X2P, M)

    def spread(c):
        for r in range(X2P // 8):
            tiles = [mixed[c * GROUP + k, 8 * r : 8 * r + 8, :] for k in range(GROUP)]
            for b in (8, 4, 2, 1):
                low = (lanes // (M3 * b)) % 2 == 0
                for k in range(GROUP):
                    if k & b == 0:
                        x, y = tiles[k], tiles[k + b]
                        tiles[k] = jnp.where(low, x, pltpu.roll(y, M3 * b, 1))
                        tiles[k + b] = jnp.where(low, pltpu.roll(x, M - M3 * b, 1), y)
            for t in range(COLS):
                send_z[c, t, 8 * r : 8 * r + 8, :] = tiles[t]

    def copy_z(c, target):
        return pltpu.make_async_remote_copy(
            src_ref=send_z.at[c, target, pl.ds(0, X2)],
            dst_ref=recv_z.at[c, pz, pl.ds(0, X2)],
            send_sem=send_z_sem.at[c],
            recv_sem=recv_z_sem.at[c],
            device_id={"pz": target},
            device_id_type=mesh,
        )

    def send_planes(c):
        for plane in PLANES:
            for core in range(2):
                target = 2 * plane + core

                @pl.when(pz != target)
                def _():
                    copy_z(c, target).start()

    def copy_y(c, step):
        target = lax.rem(py + step, ROWS)
        return pltpu.make_async_remote_copy(
            src_ref=send_y.at[c, pl.ds(M2 * target, M2)],
            dst_ref=recv_y.at[c, pl.ds(M2 * py, M2)],
            send_sem=send_y_sem.at[c],
            recv_sem=recv_y_sem.at[c],
            device_id={"py": target},
            device_id_type=mesh,
        )

    def all_z(c):
        return pltpu.make_async_remote_copy(
            src_ref=send_z.at[c, pl.ds(0, COLS - 1), pl.ds(0, X2)],
            dst_ref=recv_z.at[c, pl.ds(0, COLS - 1), pl.ds(0, X2)],
            send_sem=send_z_sem.at[c],
            recv_sem=recv_z_sem.at[c],
            device_id={"pz": lax.rem(pz + 1, COLS)},
            device_id_type=mesh,
        )

    def all_y(c):
        return pltpu.make_async_remote_copy(
            src_ref=send_y.at[c, pl.ds(0, M2 * (ROWS - 1))],
            dst_ref=recv_y.at[c, pl.ds(0, M2 * (ROWS - 1))],
            send_sem=send_y_sem.at[c],
            recv_sem=recv_y_sem.at[c],
            device_id={"py": lax.rem(py + 1, ROWS)},
            device_id_type=mesh,
        )

    third_copy.wait()
    done_x = 0
    for c in range(CHUNKS):
        while done_x < X1 and done_x * FIELDS < (c + 1) * GROUP:
            third_step(done_x)
            done_x += 1
        spread(c)
        if c == 0:
            pl.semaphore_wait(barrier, COLS + ROWS - 2)
        send_planes(c)
        recv_z[c, pz, :X2] = send_z[c, pz, :X2]

    second_copy.wait()
    for c in range(CHUNKS):
        all_z(c).wait_recv()
        send_y[c] = dot(second_ref[...], recv_z[c].reshape(COLS * X2P, M))
        for step in range(1, ROWS):
            copy_y(c, step).start()

    first_copy.wait()
    coarse = [None] * FIELDS
    place = lax.broadcasted_iota(jnp.int32, (ROWS * M2, M), 0) // M2
    for c in range(CHUNKS):
        all_y(c).wait_recv()
        turned = jnp.where(place == py, send_y[c], recv_y[c]).T
        for x in range(X1):
            begin = max(x * FIELDS, c * GROUP)
            end = min((x + 1) * FIELDS, (c + 1) * GROUP)
            if begin >= end:
                continue
            rows = turned[M3 * (begin - c * GROUP) : M3 * (end - c * GROUP)]
            own = lax.rem(lax.broadcasted_iota(jnp.int32, rows.shape, 1), M2)
            stacked = jnp.concatenate([jnp.where(own == m, rows, 0.0) for m in range(M2)], axis=0)
            done = dot(stacked, first_ref[x]).reshape(M2, end - begin, M3, M)
            for k in range(end - begin):
                f = begin + k - x * FIELDS
                if x == 0:
                    coarse_ref[f] = done[:, k]
                else:
                    coarse_ref[f] += done[:, k]

    for c in range(CHUNKS):
        all_z(c).wait_send()
        all_y(c).wait_send()


def finish(coarse_ref, filtered_ref, stress_ref):
    filtered_ref[...] = coarse_ref[:3]
    for p, (a, b) in enumerate(factor_pairs):
        stress_ref[p] = coarse_ref[3 + p] - coarse_ref[a] * coarse_ref[b]


def shards(velocity):
    third, second, first = (jnp.asarray(table, jnp.float32) for table in tables())
    vmem = pl.BlockSpec(memory_space=pltpu.VMEM)
    anywhere = pl.BlockSpec(memory_space=pl.ANY)
    f32 = jnp.float32
    coarse = pl.pallas_call(
        kernel,
        out_shape=jax.ShapeDtypeStruct((FIELDS, M2, M3, M), f32),
        in_specs=[anywhere] * 4,
        out_specs=vmem,
        scratch_shapes=[
            pltpu.VMEM((3, X1, X2, N), f32),
            pltpu.VMEM((N, M), f32),
            pltpu.VMEM((M, COLS * X2P), f32),
            pltpu.VMEM((X1, ROWS * M2, M), f32),
            pltpu.VMEM((CHUNKS * GROUP, X2P, M), f32),
            pltpu.VMEM((CHUNKS, COLS, X2P, M), f32),
            pltpu.VMEM((CHUNKS, COLS, X2P, M), f32),
            pltpu.VMEM((CHUNKS, ROWS * M2, M), f32),
            pltpu.VMEM((CHUNKS, ROWS * M2, M), f32),
            pltpu.SemaphoreType.DMA((X1,)),
            pltpu.SemaphoreType.DMA((3,)),
            pltpu.SemaphoreType.DMA((CHUNKS,)),
            pltpu.SemaphoreType.DMA((CHUNKS,)),
            pltpu.SemaphoreType.DMA((CHUNKS,)),
            pltpu.SemaphoreType.DMA((CHUNKS,)),
        ],
        compiler_params=pltpu.CompilerParams(collective_id=0, has_side_effects=True),
    )(velocity, third, second, first)
    return pl.pallas_call(
        finish,
        out_shape=(
            jax.ShapeDtypeStruct((3, M2, M3, M), f32),
            jax.ShapeDtypeStruct((6, M2, M3, M), f32),
        ),
        in_specs=[vmem],
        out_specs=(vmem, vmem),
    )(coarse)


def solution(mesh):
    placed = P(None, "py", "pz", None)
    return jax.shard_map(
        shards, mesh=mesh, in_specs=(placed,), out_specs=(placed, placed), check_vma=False
    )
```

time: 53.6 us -> 47.7 us (0.89)
  local copies, waits for them, and re-layouts: 2.96 us -> 0 us
  Pallas kernels: 49.8 us -> 46.9 us
    unnamed x2 -> x0, local copies, waits for them, and re-layouts: 2.96 us -> none
    pallas_call x1 -> x2, Pallas kernels: 49.8 us -> 46.9 us  [the longest x1 45.3 us: shards(): pl.pallas_call(kernel, out_shape=jax.ShapeDtypeStruct((FIELDS, M2, M3, M)...]
where the time goes in v2:
time: 47.7 us; the launch traced here: 47.5 us
  Pallas kernels  46.9 us (98%)
  between operations  0.64 us (1%)
    pallas_call x1, Pallas kernels, shards(): pl.pallas_call(kernel, out_shape=jax.ShapeDtypeStruct((FIELDS, M2, M3, M)...  45.3 us
    pallas_call x1, Pallas kernels, shards(): pl.pallas_call(finish, out_shape=(jax.ShapeDtypeStruct((3, M2, M3, M), f3...  1.57 us

profile of v2, /device:TPU:1, one launch (start us, length us, event | category | flops | bytes accessed | tf_op | source)
XLA Modules:
  0.0 47.5 jit_solution(6592344570951956016)
XLA Ops:
  0.6 45.3 %shard_map.59.coarse_ref = f32[9,4,8,128]{3,2,1,0:T(8,128)} custom-call(f32[3,10,20,320]{3,2,1,0:T(8,128)} %v_hbm.1, f32[320,128]{1,0:T(8,128)} %constant.6.clone.third_hbm, f32[128,384]{1,0:T(8,128)} %constant.7.clone.second_hbm, f32[10,128,128]{2,1,0:T(8,128)} %constant.8.clone.first_hbm), custom_call_target="tpu_custom_call" | custom-call | tf_op jit(solution)/shard_map/pallas_call | solution.py:233
  45.9 1.6 %shard_map.60 = (f32[3,4,8,128]{3,2,1,0:T(8,128)}, f32[6,4,8,128]{3,2,1,0:T(8,128)}) custom-call(f32[9,4,8,128]{3,2,1,0:T(8,128)} %shard_map.59.coarse_ref), custom_call_target="tpu_custom_call" | custom-call | tf_op jit(solution)/shard_map/pallas_call | solution.py:257

commit v3 on v2

--- a/solution.py
+++ b/solution.py
@@ -22,7 +22,13 @@
 M3 = M // COLS
 GROUP = 16
 CHUNKS = -(-X1 * FIELDS // GROUP)
-PLANES = (0, 1, 3, 2, 7, 4, 6, 5)
+PLANES = (0, 1, 2, 3, 7, 4, 6, 5)
+
+
+STEPS = sorted(
+    ((down, right) for down in range(8) for right in range(4) if (down, right) != (0, 0)),
+    key=lambda step: -min(step[0], 8 - step[0]) - min(step[1], 4 - step[1]),
+)
 
 
 def filter_matrix():
@@ -45,7 +51,7 @@
         a,
         b,
         (((1,), (0,)), ((), ())),
-        precision=lax.Precision.HIGH,
+        precision=lax.Precision.HIGHEST,
         preferred_element_type=jnp.float32,
     )
 
@@ -133,9 +139,9 @@
             device_id_type=mesh,
         )
 
-    def send_planes(c):
-        for plane in PLANES:
-            for core in range(2):
+    def send_planes(c, planes):
+        for plane in planes:
+            for core in (1, 0):
                 target = 2 * plane + core
 
                 @pl.when(pz != target)
@@ -143,7 +149,8 @@
                     copy_z(c, target).start()
 
     def copy_y(c, step):
-        target = lax.rem(py + step, ROWS)
+        down, right = step
+        target = 4 * lax.rem(py // 4 + down, 8) + lax.rem(lax.rem(py, 4) + right, 4)
         return pltpu.make_async_remote_copy(
             src_ref=send_y.at[c, pl.ds(M2 * target, M2)],
             dst_ref=recv_y.at[c, pl.ds(M2 * py, M2)],
@@ -182,14 +189,19 @@
         spread(c)
         if c == 0:
             pl.semaphore_wait(barrier, COLS + ROWS - 2)
-        send_planes(c)
+        if c < CHUNKS - 2:
+            send_planes(c, PLANES)
         recv_z[c, pz, :X2] = send_z[c, pz, :X2]
+
+    for planes in ((0,), (1,), (2,), (3,), (7, 4, 6, 5)):
+        for c in range(CHUNKS - 2, CHUNKS):
+            send_planes(c, planes)
 
     second_copy.wait()
     for c in range(CHUNKS):
         all_z(c).wait_recv()
         send_y[c] = dot(second_ref[...], recv_z[c].reshape(COLS * X2P, M))
-        for step in range(1, ROWS):
+        for step in STEPS:
             copy_y(c, step).start()
 
     first_copy.wait()
@@ -252,8 +264,8 @@
             pltpu.SemaphoreType.DMA((CHUNKS,)),
             pltpu.SemaphoreType.DMA((CHUNKS,)),
         ],
-        compiler_params=pltpu.CompilerParams(collective_id=0, has_side_effects=True),
-    )(velocity, third, second, first)
+        compiler_params=pltpu.CompilerParams(collective_id=0, has_side_effects=True, vmem_limit_bytes=24 << 20),
+    )(*(pltpu.with_memory_space_constraint(x, pltpu.HBM) for x in (velocity, third, second, first)))
     return pl.pallas_call(
         finish,
         out_shape=(
@@ -262,6 +274,7 @@
         ),
         in_specs=[vmem],
         out_specs=(vmem, vmem),
+        compiler_params=pltpu.CompilerParams(vmem_limit_bytes=4 << 20),
     )(coarse)
 
 

time: 47.7 us -> 45.7 us (0.958)
  the two profiles are of different devices: /device:TPU:1 before, /device:TPU:128 now
where the time goes in v3:
time: 45.7 us; the launch traced here: 45.6 us
  Pallas kernels  44.9 us (98%)
  between operations  0.64 us (1%)
    pallas_call x1, Pallas kernels, shards(): pl.pallas_call(kernel, out_shape=jax.ShapeDtypeStruct((FIELDS, M2, M3, M)...  44.3 us

profile of v3, /device:TPU:128, one launch (start us, length us, event | category | flops | bytes accessed | tf_op | source)
XLA Modules:
  0.0 45.6 jit_solution(17655783832053495034)
XLA Ops:
  0.6 44.3 %shard_map.59.coarse_ref = f32[9,4,8,128]{3,2,1,0:T(8,128)S(1)} custom-call(f32[3,10,20,320]{3,2,1,0:T(8,128)} %v_hbm.1, f32[320,128]{1,0:T(8,128)} %constant.6.clone.third_hbm, f32[128,384]{1,0:T(8,128)} %constant.7.clone.second_hbm, f32[10,128,128]{2,1,0:T(8,128)} %constant.8.clone.first_hbm), custom_call_target="tpu_custom_call" | custom-call | tf_op jit(solution)/shard_map/pallas_call | solution.py:245
  44.9 0.7 %shard_map.60 = (f32[3,4,8,128]{3,2,1,0:T(8,128)}, f32[6,4,8,128]{3,2,1,0:T(8,128)}) custom-call(f32[9,4,8,128]{3,2,1,0:T(8,128)S(1)} %shard_map.59.coarse_ref), custom_call_target="tpu_custom_call" | custom-call | tf_op jit(solution)/shard_map/pallas_call | solution.py:269

commit v4 on v3

--- a/solution.py
+++ b/solution.py
@@ -22,12 +22,15 @@
 M3 = M // COLS
 GROUP = 16
 CHUNKS = -(-X1 * FIELDS // GROUP)
+STARTS = [max(0, X1 * FIELDS - GROUP * (CHUNKS - c)) for c in range(CHUNKS + 1)]
+HALF = M3 * STARTS[1] // 2
+FOLD = 7
+FOLDS = M // HALF
 PLANES = (0, 1, 2, 3, 7, 4, 6, 5)
 
 
-STEPS = sorted(
-    ((down, right) for down in range(8) for right in range(4) if (down, right) != (0, 0)),
-    key=lambda step: -min(step[0], 8 - step[0]) - min(step[1], 4 - step[1]),
+TARGETS = sorted(
+    range(ROWS), key=lambda p: min(p // 4, 8 - p // 4) + min(p % 4, 4 - p % 4)
 )
 
 
@@ -69,6 +72,8 @@
     mixed,
     send_z,
     recv_z,
+    fold_send,
+    fold_recv,
     send_y,
     recv_y,
     v_sem,
@@ -104,7 +109,6 @@
             barrier, inc=1, device_id={"py": lax.rem(py + step, ROWS)}, device_id_type=mesh
         )
 
-    mixed[X1 * FIELDS :] = jnp.zeros((CHUNKS * GROUP - X1 * FIELDS, X2P, M), jnp.float32)
     recv_z[:, :, X2:, :] = jnp.zeros((CHUNKS, COLS, X2P - X2, M), jnp.float32)
     lanes = lax.broadcasted_iota(jnp.int32, (8, M), 1)
 
@@ -118,7 +122,9 @@
 
     def spread(c):
         for r in range(X2P // 8):
-            tiles = [mixed[c * GROUP + k, 8 * r : 8 * r + 8, :] for k in range(GROUP)]
+            pairs = range(STARTS[c], STARTS[c + 1])
+            tiles = [mixed[k, 8 * r : 8 * r + 8, :] for k in pairs]
+            tiles = tiles + [jnp.zeros((8, M), jnp.float32)] * (GROUP - len(pairs))
             for b in (8, 4, 2, 1):
                 low = (lanes // (M3 * b)) % 2 == 0
                 for k in range(GROUP):
@@ -129,7 +135,38 @@
             for t in range(COLS):
                 send_z[c, t, 8 * r : 8 * r + 8, :] = tiles[t]
 
+    def fold():
+        for t in range(COLS):
+            for half in range(2):
+                row = jnp.zeros((8, M), jnp.float32)
+                for g in range(FOLDS):
+                    part = send_z[0, t, FOLD * g : FOLD * g + 8, :]
+                    part = pltpu.roll(part, (HALF * (g - half)) % M, 1) if g != half else part
+                    row = jnp.where(lanes // HALF == g, part, row)
+                fold_send[t, FOLD * half : FOLD * half + 8, :] = row
+
+    def unfold():
+        for t in range(COLS):
+            for g in range(FOLDS):
+                row = jnp.zeros((8, M), jnp.float32)
+                for half in range(2):
+                    part = fold_recv[t, FOLD * half : FOLD * half + 8, :]
+                    part = pltpu.roll(part, (HALF * (half - g)) % M, 1) if g != half else part
+                    row = jnp.where(lanes // HALF == half, part, row)
+                kept = min(8, X2 - FOLD * g)
+                recv_z[0, t, FOLD * g : FOLD * g + kept, :] = row[:kept]
+        recv_z[0, pz, :X2] = send_z[0, pz, :X2]
+
     def copy_z(c, target):
+        if c == 0:
+            return pltpu.make_async_remote_copy(
+                src_ref=fold_send.at[target, pl.ds(0, 2 * FOLD)],
+                dst_ref=fold_recv.at[pz, pl.ds(0, 2 * FOLD)],
+                send_sem=send_z_sem.at[c],
+                recv_sem=recv_z_sem.at[c],
+                device_id={"pz": target},
+                device_id_type=mesh,
+            )
         return pltpu.make_async_remote_copy(
             src_ref=send_z.at[c, target, pl.ds(0, X2)],
             dst_ref=recv_z.at[c, pz, pl.ds(0, X2)],
@@ -141,16 +178,14 @@
 
     def send_planes(c, planes):
         for plane in planes:
-            for core in (1, 0):
+            for core in (1, 0) if plane == 0 else (0, 1):
                 target = 2 * plane + core
 
                 @pl.when(pz != target)
                 def _():
                     copy_z(c, target).start()
 
-    def copy_y(c, step):
-        down, right = step
-        target = 4 * lax.rem(py // 4 + down, 8) + lax.rem(lax.rem(py, 4) + right, 4)
+    def copy_y(c, target):
         return pltpu.make_async_remote_copy(
             src_ref=send_y.at[c, pl.ds(M2 * target, M2)],
             dst_ref=recv_y.at[c, pl.ds(M2 * py, M2)],
@@ -161,6 +196,15 @@
         )
 
     def all_z(c):
+        if c == 0:
+            return pltpu.make_async_remote_copy(
+                src_ref=fold_send.at[pl.ds(0, COLS - 1), pl.ds(0, 2 * FOLD)],
+                dst_ref=fold_recv.at[pl.ds(0, COLS - 1), pl.ds(0, 2 * FOLD)],
+                send_sem=send_z_sem.at[c],
+                recv_sem=recv_z_sem.at[c],
+                device_id={"pz": lax.rem(pz + 1, COLS)},
+                device_id_type=mesh,
+            )
         return pltpu.make_async_remote_copy(
             src_ref=send_z.at[c, pl.ds(0, COLS - 1), pl.ds(0, X2)],
             dst_ref=recv_z.at[c, pl.ds(0, COLS - 1), pl.ds(0, X2)],
@@ -183,26 +227,34 @@
     third_copy.wait()
     done_x = 0
     for c in range(CHUNKS):
-        while done_x < X1 and done_x * FIELDS < (c + 1) * GROUP:
+        while done_x * FIELDS < STARTS[c + 1]:
             third_step(done_x)
             done_x += 1
         spread(c)
         if c == 0:
+            fold()
             pl.semaphore_wait(barrier, COLS + ROWS - 2)
-        if c < CHUNKS - 2:
+        if c < CHUNKS - 1:
             send_planes(c, PLANES)
-        recv_z[c, pz, :X2] = send_z[c, pz, :X2]
-
-    for planes in ((0,), (1,), (2,), (3,), (7, 4, 6, 5)):
-        for c in range(CHUNKS - 2, CHUNKS):
+        if c > 0:
+            recv_z[c, pz, :X2] = send_z[c, pz, :X2]
+
+    for planes in ((0, 2, 1), (3, 7, 4, 6, 5)):
+        for c in range(CHUNKS - 1, CHUNKS):
             send_planes(c, planes)
 
     second_copy.wait()
     for c in range(CHUNKS):
         all_z(c).wait_recv()
+        if c == 0:
+            unfold()
         send_y[c] = dot(second_ref[...], recv_z[c].reshape(COLS * X2P, M))
-        for step in STEPS:
-            copy_y(c, step).start()
+        for target in TARGETS:
+
+            @pl.when(py != target)
+            def _():
+                copy_y(c, target).start()
+
 
     first_copy.wait()
     coarse = [None] * FIELDS
@@ -211,11 +263,11 @@
         all_y(c).wait_recv()
         turned = jnp.where(place == py, send_y[c], recv_y[c]).T
         for x in range(X1):
-            begin = max(x * FIELDS, c * GROUP)
-            end = min((x + 1) * FIELDS, (c + 1) * GROUP)
+            begin = max(x * FIELDS, STARTS[c])
+            end = min((x + 1) * FIELDS, STARTS[c + 1])
             if begin >= end:
                 continue
-            rows = turned[M3 * (begin - c * GROUP) : M3 * (end - c * GROUP)]
+            rows = turned[M3 * (begin - STARTS[c]) : M3 * (end - STARTS[c])]
             own = lax.rem(lax.broadcasted_iota(jnp.int32, rows.shape, 1), M2)
             stacked = jnp.concatenate([jnp.where(own == m, rows, 0.0) for m in range(M2)], axis=0)
             done = dot(stacked, first_ref[x]).reshape(M2, end - begin, M3, M)
@@ -252,9 +304,11 @@
             pltpu.VMEM((N, M), f32),
             pltpu.VMEM((M, COLS * X2P), f32),
             pltpu.VMEM((X1, ROWS * M2, M), f32),
-            pltpu.VMEM((CHUNKS * GROUP, X2P, M), f32),
+            pltpu.VMEM((X1 * FIELDS, X2P, M), f32),
             pltpu.VMEM((CHUNKS, COLS, X2P, M), f32),
             pltpu.VMEM((CHUNKS, COLS, X2P, M), f32),
+            pltpu.VMEM((COLS, 16, M), f32),
+            pltpu.VMEM((COLS, 16, M), f32),
             pltpu.VMEM((CHUNKS, ROWS * M2, M), f32),
             pltpu.VMEM((CHUNKS, ROWS * M2, M), f32),
             pltpu.SemaphoreType.DMA((X1,)),

time: 45.7 us -> 45.2 us (0.989)
  the two profiles are of different devices: /device:TPU:128 before, /device:TPU:1 now
where the time goes in v4:
time: 45.2 us; the launch traced here: 44.9 us
  Pallas kernels  44.3 us (98%)
  between operations  0.64 us (1%)
    pallas_call x1, Pallas kernels, shards(): pl.pallas_call(kernel, out_shape=jax.ShapeDtypeStruct((FIELDS, M2, M3, M)...  43.6 us

profile of v4, /device:TPU:1, one launch (start us, length us, event | category | flops | bytes accessed | tf_op | source)
XLA Modules:
  0.0 44.9 jit_solution(7334642642403142086)
XLA Ops:
  0.6 43.6 %shard_map.59.coarse_ref = f32[9,4,8,128]{3,2,1,0:T(8,128)S(1)} custom-call(f32[3,10,20,320]{3,2,1,0:T(8,128)} %v_hbm.1, f32[320,128]{1,0:T(8,128)} %constant.6.clone.third_hbm, f32[128,384]{1,0:T(8,128)} %constant.7.clone.second_hbm, f32[10,128,128]{2,1,0:T(8,128)} %constant.8.clone.first_hbm), custom_call_target="tpu_custom_call" | custom-call | tf_op jit(solution)/shard_map/pallas_call | solution.py:297
  44.3 0.7 %shard_map.60 = (f32[3,4,8,128]{3,2,1,0:T(8,128)}, f32[6,4,8,128]{3,2,1,0:T(8,128)}) custom-call(f32[9,4,8,128]{3,2,1,0:T(8,128)S(1)} %shard_map.59.coarse_ref), custom_call_target="tpu_custom_call" | custom-call | tf_op jit(solution)/shard_map/pallas_call | solution.py:323

commit v5 on v4

--- a/solution.py
+++ b/solution.py
@@ -69,6 +69,7 @@
     third_ref,
     second_ref,
     first_ref,
+    wide_ref,
     mixed,
     send_z,
     recv_z,
@@ -239,10 +240,15 @@
         if c > 0:
             recv_z[c, pz, :X2] = send_z[c, pz, :X2]
 
-    for planes in ((0, 2, 1), (3, 7, 4, 6, 5)):
+    for planes in ((0, 1, 2), (3, 7, 4, 6, 5)):
         for c in range(CHUNKS - 1, CHUNKS):
             send_planes(c, planes)
 
+    first_copy.wait()
+    own = lax.rem(lax.broadcasted_iota(jnp.int32, (ROWS * M2, M), 0), M2)
+    for x in range(X1):
+        for m in range(M2):
+            wide_ref[x, :, M * m : M * (m + 1)] = jnp.where(own == m, first_ref[x], 0.0)
     second_copy.wait()
     for c in range(CHUNKS):
         all_z(c).wait_recv()
@@ -256,7 +262,6 @@
                 copy_y(c, target).start()
 
 
-    first_copy.wait()
     coarse = [None] * FIELDS
     place = lax.broadcasted_iota(jnp.int32, (ROWS * M2, M), 0) // M2
     for c in range(CHUNKS):
@@ -268,15 +273,15 @@
             if begin >= end:
                 continue
             rows = turned[M3 * (begin - STARTS[c]) : M3 * (end - STARTS[c])]
-            own = lax.rem(lax.broadcasted_iota(jnp.int32, rows.shape, 1), M2)
-            stacked = jnp.concatenate([jnp.where(own == m, rows, 0.0) for m in range(M2)], axis=0)
-            done = dot(stacked, first_ref[x]).reshape(M2, end - begin, M3, M)
+            done = dot(rows, wide_ref[x])
             for k in range(end - begin):
                 f = begin + k - x * FIELDS
-                if x == 0:
-                    coarse_ref[f] = done[:, k]
-                else:
-                    coarse_ref[f] += done[:, k]
+                for m in range(M2):
+                    tile = done[M3 * k : M3 * (k + 1), M * m : M * (m + 1)]
+                    if x == 0:
+                        coarse_ref[f, m] = tile
+                    else:
+                        coarse_ref[f, m] += tile
 
     for c in range(CHUNKS):
         all_z(c).wait_send()
@@ -304,6 +309,7 @@
             pltpu.VMEM((N, M), f32),
             pltpu.VMEM((M, COLS * X2P), f32),
             pltpu.VMEM((X1, ROWS * M2, M), f32),
+            pltpu.VMEM((X1, ROWS * M2, M2 * M), f32),
             pltpu.VMEM((X1 * FIELDS, X2P, M), f32),
             pltpu.VMEM((CHUNKS, COLS, X2P, M), f32),
             pltpu.VMEM((CHUNKS, COLS, X2P, M), f32),

time: 45.2 us -> 44.9 us (level)
  no operation moved by 1% of the time
where the time goes in v5:
time: 44.9 us; the launch traced here: 44.8 us
  Pallas kernels  44.2 us (98%)
  between operations  0.64 us (1%)
    pallas_call x1, Pallas kernels, shards(): pl.pallas_call(kernel, out_shape=jax.ShapeDtypeStruct((FIELDS, M2, M3, M)...  43.5 us

profile of v5, /device:TPU:1, one launch (start us, length us, event | category | flops | bytes accessed | tf_op | source)
XLA Modules:
  0.0 44.8 jit_solution(12058981583094424744)
XLA Ops:
  0.6 43.5 %shard_map.59.coarse_ref = f32[9,4,8,128]{3,2,1,0:T(8,128)S(1)} custom-call(f32[3,10,20,320]{3,2,1,0:T(8,128)} %v_hbm.1, f32[320,128]{1,0:T(8,128)} %constant.6.clone.third_hbm, f32[128,384]{1,0:T(8,128)} %constant.7.clone.second_hbm, f32[10,128,128]{2,1,0:T(8,128)} %constant.8.clone.first_hbm), custom_call_target="tpu_custom_call" | custom-call | tf_op jit(solution)/shard_map/pallas_call | solution.py:302
  44.1 0.7 %shard_map.60 = (f32[3,4,8,128]{3,2,1,0:T(8,128)}, f32[6,4,8,128]{3,2,1,0:T(8,128)}) custom-call(f32[9,4,8,128]{3,2,1,0:T(8,128)S(1)} %shard_map.59.coarse_ref), custom_call_target="tpu_custom_call" | custom-call | tf_op jit(solution)/shard_map/pallas_call | solution.py:329

commit v6 on v5

--- a/solution.py
+++ b/solution.py
@@ -94,21 +94,21 @@
     third_copy = pltpu.make_async_copy(third_hbm, third_ref, table_sem.at[0])
     second_copy = pltpu.make_async_copy(second_hbm, second_ref, table_sem.at[1])
     first_copy = pltpu.make_async_copy(first_hbm, first_ref, table_sem.at[2])
+    barrier = pltpu.get_barrier_semaphore()
+    for step in range(1, COLS):
+        pl.semaphore_signal(
+            barrier, inc=1, device_id={"pz": lax.rem(pz + step, COLS)}, device_id_type=mesh
+        )
+    for step in range(1, ROWS):
+        pl.semaphore_signal(
+            barrier, inc=1, device_id={"py": lax.rem(py + step, ROWS)}, device_id_type=mesh
+        )
+
     third_copy.start()
     for copy in v_copies:
         copy.start()
     second_copy.start()
     first_copy.start()
-
-    barrier = pltpu.get_barrier_semaphore()
-    for step in range(1, COLS):
-        pl.semaphore_signal(
-            barrier, inc=1, device_id={"pz": lax.rem(pz + step, COLS)}, device_id_type=mesh
-        )
-    for step in range(1, ROWS):
-        pl.semaphore_signal(
-            barrier, inc=1, device_id={"py": lax.rem(py + step, ROWS)}, device_id_type=mesh
-        )
 
     recv_z[:, :, X2:, :] = jnp.zeros((CHUNKS, COLS, X2P - X2, M), jnp.float32)
     lanes = lax.broadcasted_iota(jnp.int32, (8, M), 1)

time: 44.9 us -> 45.3 us (level)
  no operation moved by 1% of the time
where the time goes in v6:
time: 45.3 us; the launch traced here: 45.1 us
  Pallas kernels  44.5 us (98%)
  between operations  0.64 us (1%)
    pallas_call x1, Pallas kernels, shards(): pl.pallas_call(kernel, out_shape=jax.ShapeDtypeStruct((FIELDS, M2, M3, M)...  43.8 us

profile of v6, /device:TPU:1, one launch (start us, length us, event | category | flops | bytes accessed | tf_op | source)
XLA Modules:
  0.0 45.1 jit_solution(17204162195906233661)
XLA Ops:
  0.6 43.8 %shard_map.59.coarse_ref = f32[9,4,8,128]{3,2,1,0:T(8,128)S(1)} custom-call(f32[3,10,20,320]{3,2,1,0:T(8,128)} %v_hbm.1, f32[320,128]{1,0:T(8,128)} %constant.6.clone.third_hbm, f32[128,384]{1,0:T(8,128)} %constant.7.clone.second_hbm, f32[10,128,128]{2,1,0:T(8,128)} %constant.8.clone.first_hbm), custom_call_target="tpu_custom_call" | custom-call | tf_op jit(solution)/shard_map/pallas_call | solution.py:302
  44.5 0.7 %shard_map.60 = (f32[3,4,8,128]{3,2,1,0:T(8,128)}, f32[6,4,8,128]{3,2,1,0:T(8,128)}) custom-call(f32[9,4,8,128]{3,2,1,0:T(8,128)S(1)} %shard_map.59.coarse_ref), custom_call_target="tpu_custom_call" | custom-call | tf_op jit(solution)/shard_map/pallas_call | solution.py:329
